TPU v7x, 256 devices: a 2x2x32 block of a 4x8x32 slice. The times are simulated.
256 devices in a mesh: reps: 4 (over x, y), grow: 64 (over z, core).
Axes of the slice: x: 2, y: 2, z: 32, core: 2. Of those that a mesh axis runs over, the one named last changes fastest.
The devices are a block of a 4x8x32 slice.
Arguments:
- hamiltonian: float32 [1536, 3, 256, 256], P(('reps', 'grow')), parts along dimension 0, may hold values from -3 to 3, as said below
- pattern: int32 [384, 3], replicated, may hold values from 0 to 1, as said below
- potential: float32 [4], P('reps'), parts along dimension 0, may hold values from -0.2 to 0.2
Outputs:
- sign_matrix: float32 [1536, 3, 256, 256], P(('reps', 'grow')), parts along dimension 0
- occupation: float32 [4], P('reps'), parts along dimension 0
There are 4 independent parts, one for each index of `reps`. A program takes and returns all parts, laid end to end along the dimension named above; an argument that names none is the same for every part. Nothing has to cross between parts.
Inputs may be any that keep to these rules, and one draw needn't show every extreme that they name: `hamiltonian`: the matrix is symmetric: slot 2 of block row i is the transpose of slot 0 of block row i + 1, slot 1 is symmetric, slot 0 of row 0 and slot 2 of row 383 are zero. pattern[i, 1] = 1; pattern[i, 2] = pattern[i + 1, 0]; pattern[0, 0] = pattern[383, 2] = 0.
All inputs are finite; a program needn't handle non-finite values.
Results may differ from a plain program's by a relative error of at most 0.0001.
Values sent between devices are 32-bit elements; how exact they have to be, the bound alone decides.
A program may use at most 64 MiB of HBM per device.

v0:
```python
import functools

import jax
import jax.numpy as jnp
from jax import lax
from jax.experimental import pallas as pl
from jax.experimental.pallas import tpu as pltpu
from jax.sharding import PartitionSpec as P

MESH = pl.DeviceIdType.MESH
F32 = jnp.float32
BF16 = jnp.bfloat16
STRIP = 32


def kernel(
    n_grow,
    pattern,
    potential,
    h_hbm,
    out,
    occupation,
    h,
    c_hi,
    c_lo,
    s_hi,
    s_lo,
    d_hi,
    d_lo,
    t_hi,
    t_lo,
    halo,
    edge,
    part,
    mate,
    slots,
    load_sem,
    send_sem,
    recv_sem,
    trace_send,
    trace_recv,
    known_sem,
):
    rows, edge_size = h.shape[0], h.shape[2]
    n_chips = n_grow // 2
    last = rows - 1
    me = lax.axis_index("grow")
    chip = me // 2
    mate_id = me + 1 - 2 * lax.rem(me, 2)

    def at(distance):
        return {"grow": lax.rem(me + distance + n_grow, n_grow)}

    loads = {}
    for i in (0, last, 1, last - 1, 2, 3):
        loads[i] = pltpu.make_async_copy(h_hbm.at[i], h.at[i], load_sem.at[i])
        loads[i].start()
    barrier = pltpu.get_barrier_semaphore()
    near = (1, -1, 2, -2, 4, -4)
    for distance in near:
        pl.semaphore_signal(barrier, inc=1, device_id=at(distance), device_id_type=MESH)
    pl.semaphore_wait(barrier, len(near))
    reaches = []
    reach = 2
    while reach < n_chips // 2:
        reaches.append(reach)
        reach *= 2

    def tell(step):
        if step >= len(reaches):
            return
        for distance in (2 * reaches[step], -2 * reaches[step]):
            pl.semaphore_signal(
                known_sem.at[step], inc=1, device_id=at(distance), device_id_type=MESH
            )

    def hear(step):
        if step >= len(reaches):
            return
        pl.semaphore_wait(known_sem.at[step], 2)

    tell(0)

    def exchange(k, first, second):
        copies = []
        for side, source, distance in ((1, first, -1), (0, second, 1)):
            copies.append(
                pltpu.make_async_remote_copy(
                    src_ref=source,
                    dst_ref=halo.at[k, side],
                    send_sem=send_sem.at[k, side],
                    recv_sem=recv_sem.at[k, side],
                    device_id=at(distance),
                    device_id_type=MESH,
                )
            )
        for copy in copies:
            copy.start()
        return copies

    first_row = me * rows
    low_mask = pattern[0, first_row].astype(F32)
    masks = [low_mask] + [pattern[2, first_row + i].astype(F32) for i in range(rows)]
    mu = potential[0]

    def strips():
        return [(r0, slice(r0, r0 + STRIP)) for r0 in range(0, edge_size, STRIP)]

    def unit(r0):
        r = lax.broadcasted_iota(jnp.int32, (STRIP, edge_size), 0) + r0
        c = lax.broadcasted_iota(jnp.int32, (STRIP, edge_size), 1)
        return r == c

    def put(dst, i, slot, strip, x):
        hi, lo = dst
        top = x.astype(BF16)
        hi[i + 1, slot, strip, :] = top
        lo[i + 1, slot, strip, :] = (x - top.astype(F32)).astype(BF16)

    def flipped(x):
        half = edge_size // 2
        top = jnp.concatenate([x[:half, :half].T, x[half:, :half].T], axis=1)
        low = jnp.concatenate([x[:half, half:].T, x[half:, half:].T], axis=1)
        return jnp.concatenate([top, low], axis=0)

    def product(terms):
        total = None
        for (a, i, s), (b, j, p) in terms:
            for left, right in ((0, 0), (1, 0), (0, 1)):
                one = jnp.dot(
                    a[left][i + 1, s], b[right][j + 1, p], preferred_element_type=F32
                )
                total = one if total is None else total + one
        return total

    def band(a, b, i, slot):
        return [
            ((a, i, s), (b, i + s - 1, slot - s + 1))
            for s in range(3)
            if 0 <= slot - s + 1 < 3
        ]

    c, s, d, t = (c_hi, c_lo), (s_hi, s_lo), (d_hi, d_lo), (t_hi, t_lo)

    def put_diagonal(i, source):
        for r0, strip in strips():
            x = jnp.where(unit(r0), mu, 0.0) - source[strip, :]
            put(c, i, 1, strip, x)

    def load_row(i):
        loads[i].wait()

    def split_row(i):
        put_diagonal(i, h.at[i, 1])
        for r0, strip in strips():
            put(c, i, 0, strip, h[i, 0, strip, :] * -masks[i])
            put(c, i, 2, strip, h[i, 2, strip, :] * -masks[i + 1])

    def mirror(i, slot, j, new_slot, mask):
        x = flipped(h[i, slot] * -mask)
        for r0, strip in strips():
            put(c, j, new_slot, strip, x[strip])

    def take_diagonal(dst, k, side, i):
        for r0, strip in strips():
            put(dst, i, 1, strip, halo[k, side, strip, :])

    def square_diagonal(dst, i, x, copy=None):
        for r0, strip in strips():
            y = jnp.where(unit(r0), 3.0, 0.0) - x[strip]
            put(dst, i, 1, strip, y)
            if copy is not None:
                copy[strip, :] = y

    def scaled(dst, i, slot, x, factor, copy=None):
        for r0, strip in strips():
            y = x[strip] * factor
            put(dst, i, slot, strip, y)
            if copy is not None:
                copy[strip, :] = y

    def symmetric_edge(i):
        x = product([((c, i, 1), (c, i, 2)), ((c, i, 2), (c, i + 1, 1))])
        x = x * -masks[i + 1]
        y = flipped(x)
        for r0, strip in strips():
            put(s, i, 2, strip, x[strip])
            put(s, i + 1, 0, strip, y[strip])

    load_row(0)
    load_row(last)
    sent = exchange(0, h.at[0, 1], h.at[last, 1])
    split_row(0)
    split_row(last)
    mirror(0, 0, -1, 2, masks[0])
    mirror(last, 2, rows, 0, masks[rows])
    load_row(1)
    load_row(last - 1)
    split_row(1)
    split_row(last - 1)
    for i in (0, last):
        side = 0 if i == 0 else 1
        square_diagonal(s, i, product(band(c, c, i, 1)), edge.at[0, side])
    sent += exchange(1, edge.at[0, 0], edge.at[0, 1])
    for i in range(2, last - 1):
        load_row(i)
    for i in range(2, last - 1):
        split_row(i)
    for i in range(1, last):
        square_diagonal(s, i, product(band(c, c, i, 1)))
    for i in range(last):
        symmetric_edge(i)
    for copy in sent[0:2]:
        copy.wait_recv()
    hear(0)
    tell(1)
    put_diagonal(-1, halo.at[0, 0])
    put_diagonal(rows, halo.at[0, 1])
    symmetric_edge(-1)
    symmetric_edge(last)

    for i in (0, last):
        side = 0 if i == 0 else 1
        scaled(d, i, 1, product(band(c, s, i, 1)), 0.5, edge.at[1, side])
    sent += exchange(2, edge.at[1, 0], edge.at[1, 1])
    half_masks = [0.5 * m for m in masks]
    for i in range(rows):
        if 0 < i < last:
            scaled(d, i, 1, product(band(c, s, i, 1)), 0.5)
        if i > 0:
            scaled(d, i, 0, product(band(c, s, i, 0)), half_masks[i])
        if i < last:
            scaled(d, i, 2, product(band(c, s, i, 2)), half_masks[i + 1])
    x = product([((c, -1, 1), (s, -1, 2)), ((c, -1, 2), (s, 0, 1))])
    scaled(d, -1, 2, x, half_masks[0])
    x = product([((c, rows, 1), (s, rows, 0)), ((c, rows, 0), (s, last, 1))])
    scaled(d, rows, 0, x, half_masks[rows])
    for copy in sent[2:4]:
        copy.wait_recv()
    hear(1)
    tell(2)
    take_diagonal(s, 1, 0, -1)
    take_diagonal(s, 1, 1, rows)
    scaled(d, 0, 0, product(band(c, s, 0, 0)), half_masks[0])
    scaled(d, last, 2, product(band(c, s, last, 2)), half_masks[rows])

    trace = jnp.zeros((8, edge_size), F32)

    def last_diagonal(i, trace, copy=None):
        own = product([((d, i, 1), (d, i, 1))])
        side = product([((d, i, 0), (d, i - 1, 2)), ((d, i, 2), (d, i + 1, 0))])
        for r0, strip in strips():
            y = jnp.where(unit(r0), 3.0, 0.0) - own[strip]
            z = side[strip]
            put(t, i, 1, strip, y - z)
            if copy is not None:
                copy[strip, :] = y - z
            a = d_hi[i + 1, 1, strip, :].astype(F32) + d_lo[i + 1, 1, strip, :].astype(F32)
            w = a * (y - 3.0 * z)
            for q in range(0, STRIP, 8):
                trace = trace + w[q : q + 8]
        return trace

    trace = last_diagonal(0, trace, edge.at[2, 0])
    trace = last_diagonal(last, trace, edge.at[2, 1])
    sent += exchange(3, edge.at[2, 0], edge.at[2, 1])
    for i in range(1, last):
        trace = last_diagonal(i, trace)
    trace = 0.5 * jnp.sum(trace, axis=0, keepdims=True)
    part[...] = trace[:, :128] + trace[:, 128:]
    pair = pltpu.make_async_remote_copy(
        src_ref=part,
        dst_ref=mate,
        send_sem=trace_send.at[0],
        recv_sem=trace_recv.at[0],
        device_id={"grow": mate_id},
        device_id_type=MESH,
    )
    pair.start()
    minus = [-m for m in masks]
    for i in range(2):
        scaled(t, i, 2, product(band(d, d, i, 2)), minus[i + 1])
    pair.wait()
    hear(2)
    slots[chip] = part[...] + mate[...]
    for k in range(1, n_chips):
        pltpu.make_async_remote_copy(
            src_ref=slots.at[chip],
            dst_ref=slots.at[chip],
            send_sem=trace_send.at[1],
            recv_sem=trace_recv.at[1],
            device_id=at(2 * k),
            device_id_type=MESH,
        ).start()
    for i in range(rows):
        if i > 0:
            scaled(t, i, 0, product(band(d, d, i, 0)), minus[i])
        if 1 < i < last:
            scaled(t, i, 2, product(band(d, d, i, 2)), minus[i + 1])
    for copy in sent[4:6]:
        copy.wait_recv()
    take_diagonal(d, 2, 0, -1)
    take_diagonal(d, 2, 1, rows)
    scaled(t, 0, 0, product(band(d, d, 0, 0)), minus[0])
    scaled(t, last, 2, product(band(d, d, last, 2)), minus[rows])
    x = product([((d, -1, 1), (d, -1, 2)), ((d, -1, 2), (d, 0, 1))])
    scaled(t, -1, 2, x, minus[0])
    x = product([((d, rows, 1), (d, rows, 0)), ((d, rows, 0), (d, last, 1))])
    scaled(t, rows, 0, x, minus[rows])

    def finish(i, slot):
        factor = 0.5 if slot == 1 else half_masks[i + slot // 2]
        out[i, slot] = product(band(d, t, i, slot)) * factor

    for i in range(rows):
        for slot in range(3):
            if (i, slot) not in ((0, 0), (last, 2)):
                finish(i, slot)
    for copy in sent[6:8]:
        copy.wait_recv()
    take_diagonal(t, 3, 0, -1)
    take_diagonal(t, 3, 1, rows)
    finish(0, 0)
    finish(last, 2)

    for copy in sent:
        copy.wait_send()
    others = slots.at[pl.ds(0, n_chips - 1)]
    for sem in (trace_send.at[1], trace_recv.at[1]):
        pltpu.make_async_copy(others, others, sem).wait()
    order = float(rows * n_grow * edge_size)
    occupation[0] = (order + jnp.sum(slots[...])) / (2.0 * order)


def local(n_grow, hamiltonian, pattern, potential):
    rows, slot_count, edge_size, _ = hamiltonian.shape
    full = (rows + 2, slot_count, edge_size, edge_size)
    block = (edge_size, edge_size)
    splits = [pltpu.VMEM(full, BF16) for _ in range(8)]
    steps = max(1, (n_grow // 2).bit_length())
    return pl.pallas_call(
        functools.partial(kernel, n_grow),
        out_shape=(
            pltpu.VMEM(hamiltonian.shape, F32),
            jax.ShapeDtypeStruct((1,), F32),
        ),
        in_specs=[
            pl.BlockSpec(memory_space=pltpu.SMEM),
            pl.BlockSpec(memory_space=pltpu.SMEM),
            pl.BlockSpec(memory_space=pltpu.HBM),
        ],
        out_specs=(
            pl.BlockSpec(memory_space=pltpu.VMEM),
            pl.BlockSpec(memory_space=pltpu.SMEM),
        ),
        scratch_shapes=[
            pltpu.VMEM(hamiltonian.shape, F32),
            *splits,
            pltpu.VMEM((4, 2, *block), F32),
            pltpu.VMEM((3, 2, *block), F32),
            pltpu.VMEM((1, 128), F32),
            pltpu.VMEM((1, 128), F32),
            pltpu.VMEM((n_grow // 2, 1, 128), F32),
            pltpu.SemaphoreType.DMA((rows,)),
            pltpu.SemaphoreType.DMA((4, 2)),
            pltpu.SemaphoreType.DMA((4, 2)),
            pltpu.SemaphoreType.DMA((2,)),
            pltpu.SemaphoreType.DMA((2,)),
            pltpu.SemaphoreType.REGULAR((steps,)),
        ],
        compiler_params=pltpu.CompilerParams(
            collective_id=0,
            has_side_effects=True,
            vmem_limit_bytes=50 * 1024 * 1024,
        ),
        cost_estimate=pl.CostEstimate(
            flops=2 * 166 * 3 * edge_size**3,
            bytes_accessed=2 * 4 * rows * slot_count * edge_size**2,
            transcendentals=0,
        ),
    )(pattern.T, potential, hamiltonian)


def solution(mesh):
    in_specs = (P(("reps", "grow"), None, None, None), P(), P("reps"))
    out_specs = (P(("reps", "grow"), None, None, None), P("reps"))
    step = functools.partial(local, mesh.shape["grow"])

    def run(hamiltonian, pattern, potential):
        return step(hamiltonian, pattern, potential)

    return jax.shard_map(run, mesh=mesh, in_specs=in_specs, out_specs=out_specs, check_vma=False)
```

profile of v0, /device:TPU:37, one launch (start us, length us, event | category | flops | bytes accessed | tf_op | source)
XLA Modules:
  0.0 58.0 jit_solution(7296560793221583367)
XLA Ops:
  1.3 52.9 %shard_map.50 = (f32[6,3,256,256]{3,2,1,0:T(8,128)S(1)}, f32[1]{0:T(128)}) custom-call(s32[3,384]{1,0:T(4,128)} %bitcast.1, f32[1]{0:T(128)S(6)} %copy.8.potential, f32[6,3,256,256]{3,2,1,0:T(8,128)} %h_hbm.1), custom_call_target="tpu_custom_call" | custom-call | flops 16710107136 | bytes 9437184 | tf_op jit(solution)/shard_map/pallas_call | solution.py:341
  54.1 2.2 %copy.7 = f32[6,3,256,256]{3,2,1,0:T(8,128)} copy(f32[6,3,256,256]{3,2,1,0:T(8,128)S(1)} %get-tuple-element.2) | data formatting | bytes 9437184
where the time goes:
time: 58.2 us; the launch traced here: 58 us
  Pallas kernels  52.9 us (91%)
  between operations  2.97 us (5%)
  local copies, waits for them, and re-layouts  2.19 us (4%)
    pallas_call x1, Pallas kernels, local(): pl.pallas_call(functools.partial(kernel, n_grow), out_shape=(pltpu.VMEM(h...  52.9 us
    unnamed x1, local copies, waits for them, and re-layouts  2.19 us

commit v1 on v0

--- a/solution.py
+++ b/solution.py
@@ -15,11 +15,12 @@
 
 def kernel(
     n_grow,
-    pattern,
+    pattern_hbm,
     potential,
     h_hbm,
     out,
     occupation,
+    pattern,
     h,
     c_hi,
     c_lo,
@@ -51,17 +52,22 @@
     def at(distance):
         return {"grow": lax.rem(me + distance + n_grow, n_grow)}
 
+    small = [
+        pltpu.make_async_copy(pattern_hbm, pattern, load_sem.at[rows]),
+    ]
     loads = {}
     for i in (0, last, 1, last - 1, 2, 3):
         loads[i] = pltpu.make_async_copy(h_hbm.at[i], h.at[i], load_sem.at[i])
         loads[i].start()
+        if i == last:
+            for copy in small:
+                copy.start()
     barrier = pltpu.get_barrier_semaphore()
-    near = (1, -1, 2, -2, 4, -4)
+    near = [sign * d for d in range(1, 9) for sign in (1, -1)]
     for distance in near:
         pl.semaphore_signal(barrier, inc=1, device_id=at(distance), device_id_type=MESH)
-    pl.semaphore_wait(barrier, len(near))
     reaches = []
-    reach = 2
+    reach = 4
     while reach < n_chips // 2:
         reaches.append(reach)
         reach *= 2
@@ -79,26 +85,39 @@
             return
         pl.semaphore_wait(known_sem.at[step], 2)
 
-    tell(0)
-
-    def exchange(k, first, second):
+    half = edge_size // 2
+    whole = [(slice(0, edge_size), slice(0, edge_size))]
+    upper = [(slice(0, half), slice(0, edge_size)), (slice(half, edge_size),) * 2]
+
+    def exchange(k, first, second, pieces):
         copies = []
-        for side, source, distance in ((1, first, -1), (0, second, 1)):
-            copies.append(
-                pltpu.make_async_remote_copy(
-                    src_ref=source,
-                    dst_ref=halo.at[k, side],
-                    send_sem=send_sem.at[k, side],
-                    recv_sem=recv_sem.at[k, side],
-                    device_id=at(distance),
-                    device_id_type=MESH,
+        for n, (r, c) in enumerate(pieces):
+            for side, source, distance in ((1, first, -1), (0, second, 1)):
+                copies.append(
+                    pltpu.make_async_remote_copy(
+                        src_ref=source.at[r, c],
+                        dst_ref=halo.at[k, side, r, c],
+                        send_sem=send_sem.at[k, side, n],
+                        recv_sem=recv_sem.at[k, side, n],
+                        device_id=at(distance),
+                        device_id_type=MESH,
+                    )
                 )
-            )
         for copy in copies:
             copy.start()
         return copies
 
+    def arrived(copies, k, pieces):
+        for copy in copies:
+            copy.wait_recv()
+        if pieces is upper:
+            for side in range(2):
+                block = halo.at[k, side]
+                block[half:, :half] = block[:half, half:].T
+
     first_row = me * rows
+    for copy in small:
+        copy.wait()
     low_mask = pattern[0, first_row].astype(F32)
     masks = [low_mask] + [pattern[2, first_row + i].astype(F32) for i in range(rows)]
     mu = potential[0]
@@ -118,7 +137,6 @@
         lo[i + 1, slot, strip, :] = (x - top.astype(F32)).astype(BF16)
 
     def flipped(x):
-        half = edge_size // 2
         top = jnp.concatenate([x[:half, :half].T, x[half:, :half].T], axis=1)
         low = jnp.concatenate([x[:half, half:].T, x[half:, half:].T], axis=1)
         return jnp.concatenate([top, low], axis=0)
@@ -150,11 +168,16 @@
     def load_row(i):
         loads[i].wait()
 
+    def split(i, slot):
+        if slot == 1:
+            put_diagonal(i, h.at[i, 1])
+        else:
+            for r0, strip in strips():
+                put(c, i, slot, strip, h[i, slot, strip, :] * -masks[i + slot // 2])
+
     def split_row(i):
-        put_diagonal(i, h.at[i, 1])
-        for r0, strip in strips():
-            put(c, i, 0, strip, h[i, 0, strip, :] * -masks[i])
-            put(c, i, 2, strip, h[i, 2, strip, :] * -masks[i + 1])
+        for slot in range(3):
+            split(i, slot)
 
     def mirror(i, slot, j, new_slot, mask):
         x = flipped(h[i, slot] * -mask)
@@ -189,60 +212,66 @@
 
     load_row(0)
     load_row(last)
-    sent = exchange(0, h.at[0, 1], h.at[last, 1])
     split_row(0)
     split_row(last)
     mirror(0, 0, -1, 2, masks[0])
     mirror(last, 2, rows, 0, masks[rows])
     load_row(1)
     load_row(last - 1)
-    split_row(1)
-    split_row(last - 1)
+    for i in (1, last - 1):
+        split_row(i)
     for i in (0, last):
         side = 0 if i == 0 else 1
         square_diagonal(s, i, product(band(c, c, i, 1)), edge.at[0, side])
-    sent += exchange(1, edge.at[0, 0], edge.at[0, 1])
+    symmetric_edge(0)
+    symmetric_edge(last - 1)
+    pl.semaphore_wait(barrier, len(near))
+    tell(0)
+    sent0 = exchange(0, h.at[0, 1], h.at[last, 1], upper)
+    sent1 = exchange(1, edge.at[0, 0], edge.at[0, 1], upper)
     for i in range(2, last - 1):
         load_row(i)
+
+    half_masks = [0.5 * m for m in masks]
+
+    def step(i, slot, copy=None):
+        factor = 0.5 if slot == 1 else half_masks[i + slot // 2]
+        scaled(d, i, slot, product(band(c, s, i, slot)), factor, copy)
+
     for i in range(2, last - 1):
         split_row(i)
     for i in range(1, last):
         square_diagonal(s, i, product(band(c, c, i, 1)))
-    for i in range(last):
+    for i in range(1, last - 1):
         symmetric_edge(i)
-    for copy in sent[0:2]:
-        copy.wait_recv()
+    step(0, 2)
+    step(1, 0)
+    step(1, 1)
+    step(1, 2)
     hear(0)
     tell(1)
+    for i in range(2, rows):
+        for slot in range(3):
+            if i < last or slot == 0:
+                step(i, slot)
+    arrived(sent0, 0, upper)
+
     put_diagonal(-1, halo.at[0, 0])
     put_diagonal(rows, halo.at[0, 1])
     symmetric_edge(-1)
     symmetric_edge(last)
-
-    for i in (0, last):
-        side = 0 if i == 0 else 1
-        scaled(d, i, 1, product(band(c, s, i, 1)), 0.5, edge.at[1, side])
-    sent += exchange(2, edge.at[1, 0], edge.at[1, 1])
-    half_masks = [0.5 * m for m in masks]
-    for i in range(rows):
-        if 0 < i < last:
-            scaled(d, i, 1, product(band(c, s, i, 1)), 0.5)
-        if i > 0:
-            scaled(d, i, 0, product(band(c, s, i, 0)), half_masks[i])
-        if i < last:
-            scaled(d, i, 2, product(band(c, s, i, 2)), half_masks[i + 1])
+    step(0, 1, edge.at[1, 0])
+    step(last, 1, edge.at[1, 1])
     x = product([((c, -1, 1), (s, -1, 2)), ((c, -1, 2), (s, 0, 1))])
     scaled(d, -1, 2, x, half_masks[0])
     x = product([((c, rows, 1), (s, rows, 0)), ((c, rows, 0), (s, last, 1))])
     scaled(d, rows, 0, x, half_masks[rows])
-    for copy in sent[2:4]:
-        copy.wait_recv()
-    hear(1)
-    tell(2)
+    sent2 = exchange(2, edge.at[1, 0], edge.at[1, 1], upper)
+    arrived(sent1, 1, upper)
     take_diagonal(s, 1, 0, -1)
     take_diagonal(s, 1, 1, rows)
-    scaled(d, 0, 0, product(band(c, s, 0, 0)), half_masks[0])
-    scaled(d, last, 2, product(band(c, s, last, 2)), half_masks[rows])
+    step(0, 0)
+    step(last, 2)
 
     trace = jnp.zeros((8, edge_size), F32)
 
@@ -261,71 +290,61 @@
                 trace = trace + w[q : q + 8]
         return trace
 
+    for i in range(1, last):
+        trace = last_diagonal(i, trace)
     trace = last_diagonal(0, trace, edge.at[2, 0])
     trace = last_diagonal(last, trace, edge.at[2, 1])
-    sent += exchange(3, edge.at[2, 0], edge.at[2, 1])
-    for i in range(1, last):
-        trace = last_diagonal(i, trace)
     trace = 0.5 * jnp.sum(trace, axis=0, keepdims=True)
     part[...] = trace[:, :128] + trace[:, 128:]
-    pair = pltpu.make_async_remote_copy(
-        src_ref=part,
-        dst_ref=mate,
-        send_sem=trace_send.at[0],
-        recv_sem=trace_recv.at[0],
-        device_id={"grow": mate_id},
-        device_id_type=MESH,
-    )
-    pair.start()
     minus = [-m for m in masks]
-    for i in range(2):
-        scaled(t, i, 2, product(band(d, d, i, 2)), minus[i + 1])
-    pair.wait()
-    hear(2)
-    slots[chip] = part[...] + mate[...]
-    for k in range(1, n_chips):
+
+    def inner(i, slot):
+        scaled(t, i, slot, product(band(d, d, i, slot)), minus[i + slot // 2])
+
+    inside = [(i, slot) for i in range(rows) for slot in (0, 2) if 0 <= i + slot - 1 < rows]
+    hear(1)
+    slots[me] = part[...]
+    for k in sorted(range(1, n_grow), key=lambda k: -min(k, n_grow - k)):
         pltpu.make_async_remote_copy(
-            src_ref=slots.at[chip],
-            dst_ref=slots.at[chip],
+            src_ref=slots.at[me],
+            dst_ref=slots.at[me],
             send_sem=trace_send.at[1],
             recv_sem=trace_recv.at[1],
-            device_id=at(2 * k),
+            device_id=at(k),
             device_id_type=MESH,
         ).start()
+    sent3 = exchange(3, edge.at[2, 0], edge.at[2, 1], whole)
+    for i, slot in inside:
+        inner(i, slot)
+
+    def finish(i, slot):
+        factor = 0.5 if slot == 1 else half_masks[i + slot // 2]
+        out[i, slot] = product(band(d, t, i, slot)) * factor
+
     for i in range(rows):
-        if i > 0:
-            scaled(t, i, 0, product(band(d, d, i, 0)), minus[i])
-        if 1 < i < last:
-            scaled(t, i, 2, product(band(d, d, i, 2)), minus[i + 1])
-    for copy in sent[4:6]:
-        copy.wait_recv()
+        for slot in range(3):
+            if 0 < i < last or (i, slot) in ((0, 2), (last, 0)):
+                finish(i, slot)
+    arrived(sent2, 2, upper)
     take_diagonal(d, 2, 0, -1)
     take_diagonal(d, 2, 1, rows)
-    scaled(t, 0, 0, product(band(d, d, 0, 0)), minus[0])
-    scaled(t, last, 2, product(band(d, d, last, 2)), minus[rows])
     x = product([((d, -1, 1), (d, -1, 2)), ((d, -1, 2), (d, 0, 1))])
     scaled(t, -1, 2, x, minus[0])
     x = product([((d, rows, 1), (d, rows, 0)), ((d, rows, 0), (d, last, 1))])
     scaled(t, rows, 0, x, minus[rows])
-
-    def finish(i, slot):
-        factor = 0.5 if slot == 1 else half_masks[i + slot // 2]
-        out[i, slot] = product(band(d, t, i, slot)) * factor
-
-    for i in range(rows):
-        for slot in range(3):
-            if (i, slot) not in ((0, 0), (last, 2)):
-                finish(i, slot)
-    for copy in sent[6:8]:
-        copy.wait_recv()
+    scaled(t, 0, 0, product(band(d, d, 0, 0)), minus[0])
+    scaled(t, last, 2, product(band(d, d, last, 2)), minus[rows])
+    finish(0, 1)
+    finish(last, 1)
+    arrived(sent3, 3, whole)
     take_diagonal(t, 3, 0, -1)
     take_diagonal(t, 3, 1, rows)
     finish(0, 0)
     finish(last, 2)
 
-    for copy in sent:
+    for copy in sent0 + sent1 + sent2 + sent3:
         copy.wait_send()
-    others = slots.at[pl.ds(0, n_chips - 1)]
+    others = slots.at[pl.ds(0, n_grow - 1)]
     for sem in (trace_send.at[1], trace_recv.at[1]):
         pltpu.make_async_copy(others, others, sem).wait()
     order = float(rows * n_grow * edge_size)
@@ -345,7 +364,7 @@
             jax.ShapeDtypeStruct((1,), F32),
         ),
         in_specs=[
-            pl.BlockSpec(memory_space=pltpu.SMEM),
+            pl.BlockSpec(memory_space=pltpu.HBM),
             pl.BlockSpec(memory_space=pltpu.SMEM),
             pl.BlockSpec(memory_space=pltpu.HBM),
         ],
@@ -354,16 +373,17 @@
             pl.BlockSpec(memory_space=pltpu.SMEM),
         ),
         scratch_shapes=[
+            pltpu.SMEM(pattern.shape[::-1], jnp.int32),
             pltpu.VMEM(hamiltonian.shape, F32),
             *splits,
             pltpu.VMEM((4, 2, *block), F32),
             pltpu.VMEM((3, 2, *block), F32),
             pltpu.VMEM((1, 128), F32),
             pltpu.VMEM((1, 128), F32),
-            pltpu.VMEM((n_grow // 2, 1, 128), F32),
-            pltpu.SemaphoreType.DMA((rows,)),
-            pltpu.SemaphoreType.DMA((4, 2)),
-            pltpu.SemaphoreType.DMA((4, 2)),
+            pltpu.VMEM((n_grow, 1, 128), F32),
+            pltpu.SemaphoreType.DMA((rows + 1,)),
+            pltpu.SemaphoreType.DMA((4, 2, 2)),
+            pltpu.SemaphoreType.DMA((4, 2, 2)),
             pltpu.SemaphoreType.DMA((2,)),
             pltpu.SemaphoreType.DMA((2,)),
             pltpu.SemaphoreType.REGULAR((steps,)),

time: 58.2 us -> 53 us (0.911)
  Pallas kernels: 52.9 us -> 47.7 us
    pallas_call x1, Pallas kernels: 52.9 us -> 47.7 us  [local(): pl.pallas_call(functools.partial(kernel, n_grow), out_shape=(pltpu.VMEM(h...]
where the time goes in v1:
time: 53 us; the launch traced here: 52.9 us
  Pallas kernels  47.7 us (90%)
  between operations  2.97 us (6%)
  local copies, waits for them, and re-layouts  2.19 us (4%)
    pallas_call x1, Pallas kernels, local(): pl.pallas_call(functools.partial(kernel, n_grow), out_shape=(pltpu.VMEM(h...  47.7 us
    unnamed x1, local copies, waits for them, and re-layouts  2.19 us

profile of v1, /device:TPU:37, one launch (start us, length us, event | category | flops | bytes accessed | tf_op | source)
XLA Modules:
  0.0 52.9 jit_solution(4448212213264092610)
XLA Ops:
  1.3 47.7 %shard_map.50 = (f32[6,3,256,256]{3,2,1,0:T(8,128)S(1)}, f32[1]{0:T(128)}) custom-call(s32[3,384]{1,0:T(4,128)} %bitcast.1, f32[1]{0:T(128)S(6)} %copy.8.potential, f32[6,3,256,256]{3,2,1,0:T(8,128)} %h_hbm.1), custom_call_target="tpu_custom_call" | custom-call | flops 16710107136 | bytes 9437184 | tf_op jit(solution)/shard_map/pallas_call | solution.py:360
  49.0 2.2 %copy.7 = f32[6,3,256,256]{3,2,1,0:T(8,128)} copy(f32[6,3,256,256]{3,2,1,0:T(8,128)S(1)} %get-tuple-element.2) | data formatting | bytes 9437184

commit v2 on v1

--- a/solution.py
+++ b/solution.py
@@ -210,14 +210,12 @@
             put(s, i, 2, strip, x[strip])
             put(s, i + 1, 0, strip, y[strip])
 
-    load_row(0)
-    load_row(last)
+    for i in (0, last, 1, last - 1):
+        load_row(i)
     split_row(0)
     split_row(last)
     mirror(0, 0, -1, 2, masks[0])
     mirror(last, 2, rows, 0, masks[rows])
-    load_row(1)
-    load_row(last - 1)
     for i in (1, last - 1):
         split_row(i)
     for i in (0, last):
@@ -361,7 +359,7 @@
         functools.partial(kernel, n_grow),
         out_shape=(
             pltpu.VMEM(hamiltonian.shape, F32),
-            jax.ShapeDtypeStruct((1,), F32),
+            pltpu.SMEM((1,), F32),
         ),
         in_specs=[
             pl.BlockSpec(memory_space=pltpu.HBM),

time: 53 us -> 51.5 us (0.972)
  between operations: 2.97 us -> 1.8 us
where the time goes in v2:
time: 51.5 us; the launch traced here: 51.4 us
  Pallas kernels  47.4 us (92%)
  local copies, waits for them, and re-layouts  2.19 us (4%)
  between operations  1.8 us (3%)
    pallas_call x1, Pallas kernels, local(): pl.pallas_call(functools.partial(kernel, n_grow), out_shape=(pltpu.VMEM(h...  47.4 us
    unnamed x1, local copies, waits for them, and re-layouts  2.19 us

profile of v2, /device:TPU:37, one launch (start us, length us, event | category | flops | bytes accessed | tf_op | source)
XLA Modules:
  0.0 51.4 jit_solution(16310429961689476689)
XLA Ops:
  1.3 47.4 %shard_map.50 = (f32[6,3,256,256]{3,2,1,0:T(8,128)S(1)}, f32[1]{0:T(128)S(4)}) custom-call(s32[3,384]{1,0:T(4,128)} %bitcast.1, f32[1]{0:T(128)S(6)} %copy.9.potential, f32[6,3,256,256]{3,2,1,0:T(8,128)} %h_hbm.1), custom_call_target="tpu_custom_call" | custom-call | flops 16710107136 | bytes 9437184 | tf_op jit(solution)/shard_map/pallas_call | solution.py:358
  49.2 2.2 %copy.7 = f32[6,3,256,256]{3,2,1,0:T(8,128)} copy(f32[6,3,256,256]{3,2,1,0:T(8,128)S(1)} %get-tuple-element.2) | data formatting | bytes 9437184

commit v3 on v2

--- a/solution.py
+++ b/solution.py
@@ -11,6 +11,7 @@
 F32 = jnp.float32
 BF16 = jnp.bfloat16
 STRIP = 32
+BEFORE = 5
 
 
 def kernel(
@@ -243,15 +244,13 @@
     for i in range(1, last - 1):
         symmetric_edge(i)
     step(0, 2)
-    step(1, 0)
-    step(1, 1)
-    step(1, 2)
+    near_rows = [(i, slot) for i in range(1, rows) for slot in range(3) if i < last or slot == 0]
+    for i, slot in near_rows[:BEFORE]:
+        step(i, slot)
     hear(0)
     tell(1)
-    for i in range(2, rows):
-        for slot in range(3):
-            if i < last or slot == 0:
-                step(i, slot)
+    for i, slot in near_rows[BEFORE:]:
+        step(i, slot)
     arrived(sent0, 0, upper)
 
     put_diagonal(-1, halo.at[0, 0])

time: 51.5 us -> 51.5 us (level)
  no operation moved by 1% of the time
where the time goes in v3:
time: 51.5 us; the launch traced here: 51.4 us
  Pallas kernels  47.4 us (92%)
  local copies, waits for them, and re-layouts  2.19 us (4%)
  between operations  1.8 us (3%)
    pallas_call x1, Pallas kernels, local(): pl.pallas_call(functools.partial(kernel, n_grow), out_shape=(pltpu.VMEM(h...  47.4 us
    unnamed x1, local copies, waits for them, and re-layouts  2.19 us

profile of v3, /device:TPU:37, one launch (start us, length us, event | category | flops | bytes accessed | tf_op | source)
XLA Modules:
  0.0 51.4 jit_solution(9219669327706747172)
XLA Ops:
  1.3 47.4 %shard_map.50 = (f32[6,3,256,256]{3,2,1,0:T(8,128)S(1)}, f32[1]{0:T(128)S(4)}) custom-call(s32[3,384]{1,0:T(4,128)} %bitcast.1, f32[1]{0:T(128)S(6)} %copy.9.potential, f32[6,3,256,256]{3,2,1,0:T(8,128)} %h_hbm.1), custom_call_target="tpu_custom_call" | custom-call | flops 16710107136 | bytes 9437184 | tf_op jit(solution)/shard_map/pallas_call | solution.py:357
  49.2 2.2 %copy.7 = f32[6,3,256,256]{3,2,1,0:T(8,128)} copy(f32[6,3,256,256]{3,2,1,0:T(8,128)S(1)} %get-tuple-element.2) | data formatting | bytes 9437184
